TPU v7x, 32 devices: a whole 2x2x4 slice. The times are simulated.
32 devices in a mesh: ep: 4 (over z), fsdp: 8 (over y, x, core).
Axes of the slice: x: 2, y: 2, z: 4, core: 2. Of those that a mesh axis runs over, the one named last changes fastest.
Arguments:
- train_gate: float32 [64, 2048, 1408], P('ep', 'fsdp'), may hold values from -0.1875 to 0.1875
- train_up: float32 [64, 2048, 1408], P('ep', 'fsdp'), may hold values from -0.1875 to 0.1875
- train_down: float32 [64, 1408, 2048], P('ep', None, 'fsdp'), may hold values from -0.21875 to 0.21875
- router_weight: float32 [2048, 64], P('fsdp', 'ep'), may hold values from -0.125 to 0.125
- router_gain: float32 [2048], P('fsdp'), may hold values from 0.25 to 1.75
Outputs:
- ready_gate: bfloat16 [64, 2048, 1408], P('ep', None, 'fsdp')
- ready_up: bfloat16 [64, 2048, 1408], P('ep', None, 'fsdp')
- ready_down: bfloat16 [64, 1408, 2048], P('ep', 'fsdp')
- scale_gate: float32 [64, 1408], P('ep', 'fsdp')
- scale_up: float32 [64, 1408], P('ep', 'fsdp')
- scale_down: float32 [64, 1408], P('ep', 'fsdp')
- serve_router: bfloat16 [2048, 64], replicated
All inputs are finite; a program needn't handle non-finite values.
Results may differ from a plain program's by a relative error of at most 0.001.
Values may be sent and summed in bfloat16 or wider, within the bound.
A program may use at most 192 MiB of HBM per device.

v0:
```python
import jax
import jax.numpy as jnp
from jax import lax
from jax.sharding import PartitionSpec as P


def body(train_gate, train_up, train_down, router_weight, router_gain):
    total_gate, total_up, total_down = lax.psum(
        (
            jnp.sum(train_gate * train_gate, axis=1),
            jnp.sum(train_up * train_up, axis=1),
            jnp.sum(train_down * train_down, axis=2),
        ),
        "fsdp",
    )
    scale_gate = jnp.sqrt(total_gate)
    scale_up = jnp.sqrt(total_up)
    scale_down = jnp.sqrt(total_down)
    narrow_gate, narrow_up, narrow_down = (
        (train_gate / jnp.expand_dims(scale_gate, 1)).astype(jnp.bfloat16),
        (train_up / jnp.expand_dims(scale_up, 1)).astype(jnp.bfloat16),
        (train_down / jnp.expand_dims(scale_down, 2)).astype(jnp.bfloat16),
    )
    ready_gate, ready_up = (
        lax.all_to_all(narrow_gate, "fsdp", split_axis=2, concat_axis=1, tiled=True),
        lax.all_to_all(narrow_up, "fsdp", split_axis=2, concat_axis=1, tiled=True),
    )
    ready_down = lax.all_to_all(narrow_down, "fsdp", split_axis=1, concat_axis=2, tiled=True)
    scale_gate = lax.dynamic_slice_in_dim(
        scale_gate, lax.axis_index("fsdp") * ready_gate.shape[2], ready_gate.shape[2], axis=1
    )
    scale_up = lax.dynamic_slice_in_dim(
        scale_up, lax.axis_index("fsdp") * ready_up.shape[2], ready_up.shape[2], axis=1
    )
    scale_down = lax.dynamic_slice_in_dim(
        scale_down, lax.axis_index("fsdp") * ready_down.shape[1], ready_down.shape[1], axis=1
    )
    part_router = (router_weight * router_gain[:, None]).astype(jnp.bfloat16)
    row_router = lax.all_gather(part_router, "fsdp", axis=0, tiled=True)
    serve_router = lax.all_gather(row_router, "ep", axis=1, tiled=True)
    return (ready_gate, ready_up, ready_down, scale_gate, scale_up, scale_down, serve_router)


def solution(mesh):
    return jax.shard_map(
        body,
        mesh=mesh,
        in_specs=(
            P("ep", "fsdp", None),
            P("ep", "fsdp", None),
            P("ep", None, "fsdp"),
            P("fsdp", "ep"),
            P("fsdp"),
        ),
        out_specs=(
            P("ep", None, "fsdp"),
            P("ep", None, "fsdp"),
            P("ep", "fsdp", None),
            P("ep", "fsdp"),
            P("ep", "fsdp"),
            P("ep", "fsdp"),
            P(),
        ),
        check_vma=False,
    )
```

profile of v0, /device:TPU:0, one launch (start us, length us, event | category | flops | bytes accessed | tf_op | source)
XLA Modules:
  0.0 618.1 jit_solution(2208627624309375978)
XLA Ops:
  7.2 9.2 %multiply_reduce_fusion = f32[16,1408]{1,0:T(8,128)} fusion(f32[16,1408,256]{2,1,0:T(8,128)} %param.7), kind=kLoop, calls=%fused_computation.2 | loop fusion | flops 11511808 | bytes 23158784 | tf_op jit(solution)/shard_map/reduce_sum | solution.py:12
  16.4 5.0 copy-done
  21.4 11.0 %multiply_reduce_fusion.1 = (f32[16,1408]{1,0:T(8,128)}, f32[16,1408]{1,0:T(8,128)}) fusion(f32[16,256,1408]{2,1,0:T(8,128)S(1)} %copy-done, f32[16,256,1408]{2,1,0:T(8,128)} %param.5), kind=kLoop, calls=%fused_computation.4 | loop fusion | flops 23023616 | bytes 46317568 | tf_op jit(solution)/shard_map/reduce_sum | solution.py:11
  32.5 23.7 %copy.28 = f32[16,256,1408]{1,0,2:T(8,128)} copy(f32[16,256,1408]{2,1,0:T(8,128)} %param.6) | data formatting | bytes 46137344 | tf_op args[1]
  56.2 32.6 %all-reduce.3.cloned.1.call-done = (f32[16,1408]{1,0:T(8,128)}, f32[16,1408]{1,0:T(8,128)}, f32[16,1408]{1,0:T(8,128)}) async-done(((f32[16,1408]{1,0:T(8,128)}, f32[16,1408]{1,0:T(8,128)}, f32[16,1408]{1,0:T(8,128)}), (f32[16,1408]{1,0:T(8,128)}, f32[16,1408]{1,0:T(8,128)}, f32[16,1408]{1,0:T(8,128)})) %all-reduce.3.cloned.1.call-update) | async-done | bytes 270352 | tf_op jit(solution)/shard_map/psum | solution.py:8
  88.8 0.9 sqrt.10
  90.0 14.2 %divide_convert_fusion = bf16[16,256,1408]{1,0,2:T(8,128)(2,1)} fusion(f32[16,256,1408]{1,0,2:T(8,128)} %copy.28, f32[16,1408]{0,1:T(8,128)S(1)} %copy.27), kind=kLoop, calls=%fused_computation.3 | loop fusion | flops 11534336 | bytes 34693120 | tf_op jit(solution)/shard_map/convert_element_type | solution.py:21
  104.2 5.2 all-to-all-start.1
  109.5 23.7 %copy.24 = f32[16,256,1408]{1,0,2:T(8,128)} copy(f32[16,256,1408]{2,1,0:T(8,128)} %param.5) | data formatting | bytes 46137344 | tf_op args[0]
  133.5 14.2 %divide_convert_fusion.1 = bf16[16,256,1408]{1,0,2:T(8,128)(2,1)} fusion(f32[16,256,1408]{1,0,2:T(8,128)} %copy.24, f32[16,1408]{0,1:T(8,128)S(1)} %copy.23), kind=kLoop, calls=%fused_computation.5 | loop fusion | flops 11534336 | bytes 34693120 | tf_op jit(solution)/shard_map/convert_element_type | solution.py:20
  147.7 89.5 %all-to-all-done.1 = bf16[16,256,1408]{1,0,2:T(8,128)(2,1)} async-done(((bf16[16,256,1408]{1,0,2:T(8,128)(2,1)}), bf16[16,256,1408]{1,0,2:T(8,128)(2,1)}, u32[]{:S(2)}, u32[]{:S(2)}) %all-to-all-start.1) | async-done | bytes 11534368 | tf_op jit(solution)/shard_map/all_to_all | solution.py:26
  237.2 5.3 all-to-all-start
  242.8 32.6 %fusion = bf16[16,1408,256]{2,0,1:T(8,128)(2,1)} fusion(f32[16,1408,256]{2,1,0:T(8,128)} %param.7, f32[16,1408]{0,1:T(8,128)S(1)} %copy.31), kind=kLoop, calls=%fused_computation.1 | loop fusion | flops 11534336 | bytes 34693120 | tf_op jit(solution)/shard_map/convert_element_type | solution.py:22
  275.4 94.8 %all-to-all-done = bf16[16,256,1408]{1,0,2:T(8,128)(2,1)} async-done(((bf16[16,256,1408]{1,0,2:T(8,128)(2,1)}), bf16[16,256,1408]{1,0,2:T(8,128)(2,1)}, u32[]{:S(2)}, u32[]{:S(2)}) %all-to-all-start) | async-done | bytes 11534368 | tf_op jit(solution)/shard_map/all_to_all | solution.py:25
  370.2 5.3 all-to-all-start.2
  375.5 130.9 %all_gather.6 = bf16[2048,16]{0,1:T(8,128)(2,1)S(1)} all-gather(bf16[256,16]{0,1:T(8,128)(2,1)S(1)} %multiply_convert_fusion), channel_id=1, replica_groups=mesh['ep'=4,'fsdp'=8] {'fsdp'}, dimensions={0}, use_global_device_ids=true | all-gather | bytes 73728 | tf_op jit(solution)/shard_map/all_gather | solution.py:39
  506.4 14.2 %all_gather.7 = bf16[2048,64]{0,1:T(8,128)(2,1)S(1)} all-gather(bf16[2048,16]{0,1:T(8,128)(2,1)S(1)} %all_gather.6), channel_id=1, replica_groups=mesh['ep'=4,'fsdp'=8] {'ep'}, dimensions={1}, use_global_device_ids=true | all-gather | bytes 327680 | tf_op jit(solution)/shard_map/all_gather | solution.py:40
  522.6 11.3 %copy.30 = bf16[16,8,256,176]{2,1,3,0:T(8,128)(2,1)} copy(bf16[16,8,256,176]{2,0,3,1:T(8,128)(2,1)} %bitcast.5) | data formatting | bytes 23068672 | tf_op jit(solution)/shard_map/all_to_all | solution.py:26
  534.0 18.0 %all_to_all.46 = bf16[16,2048,176]{1,2,0:T(8,128)(2,1)} reshape(bf16[16,8,256,176]{2,1,3,0:T(8,128)(2,1)} %copy.30) | data formatting | bytes 23068672 | tf_op jit(solution)/shard_map/all_to_all | solution.py:26
  551.9 11.3 %copy.26 = bf16[16,8,256,176]{2,1,3,0:T(8,128)(2,1)} copy(bf16[16,8,256,176]{2,0,3,1:T(8,128)(2,1)} %bitcast.2) | data formatting | bytes 23068672 | tf_op jit(solution)/shard_map/all_to_all | solution.py:25
  563.3 18.0 %all_to_all.42 = bf16[16,2048,176]{1,2,0:T(8,128)(2,1)} reshape(bf16[16,8,256,176]{2,1,3,0:T(8,128)(2,1)} %copy.26) | data formatting | bytes 23068672 | tf_op jit(solution)/shard_map/all_to_all | solution.py:25
  581.2 11.3 %copy.33 = bf16[16,176,8,256]{3,2,1,0:T(8,128)(2,1)} copy(bf16[16,176,8,256]{3,0,1,2:T(8,128)(2,1)} %bitcast.7) | data formatting | bytes 23068672 | tf_op jit(solution)/shard_map/all_to_all | solution.py:28
  592.5 18.0 %all_to_all.50 = bf16[16,176,2048]{2,1,0:T(8,128)(2,1)} reshape(bf16[16,176,8,256]{3,2,1,0:T(8,128)(2,1)} %copy.33) | data formatting | bytes 23068672 | tf_op jit(solution)/shard_map/all_to_all | solution.py:28
  610.5 0.7 copy.43
  (21 shorter events, 3.0 us)
Async XLA Ops:
  7.2 81.6 %all-reduce.3.cloned.1.call-start = ((), (), s32[]{:S(2)}) async-start(), calls=%async_computation.3 | async-start | bytes 540672 | tf_op jit(solution)/shard_map/psum | solution.py:8
  7.2 14.2 %copy-start = (f32[16,256,1408]{2,1,0:T(8,128)S(1)}, f32[16,256,1408]{2,1,0:T(8,128)}, u32[]{:S(2)}) copy-start(f32[16,256,1408]{2,1,0:T(8,128)} %param.6) | copy-start | bytes 69206016
  104.2 133.0 %all-to-all-start.1 = ((bf16[16,256,1408]{1,0,2:T(8,128)(2,1)}), bf16[16,256,1408]{1,0,2:T(8,128)(2,1)}, u32[]{:S(2)}, u32[]{:S(2)}) async-start(bf16[16,256,1408]{1,0,2:T(8,128)(2,1)} %divide_convert_fusion), calls=%async_computation.1 | async-start | bytes 23068672 | tf_op jit(solution)/shard_map/all_to_all | solution.py:26
  109.5 23.7 %copy-start.2 = (f32[16,1408]{1,0:T(8,128)S(1)}, f32[16,1408]{1,0:T(8,128)}, u32[]{:S(2)}) copy-start(f32[16,1408]{1,0:T(8,128)} %get-tuple-element.7) | copy-start | bytes 270340
  133.5 109.0 %copy-start.1 = (f32[16,1408]{1,0:T(8,128)S(1)}, f32[16,1408]{1,0:T(8,128)}, u32[]{:S(2)}) copy-start(f32[16,1408]{1,0:T(8,128)} %get-tuple-element.9) | copy-start | bytes 270340
  237.2 133.0 %all-to-all-start = ((bf16[16,256,1408]{1,0,2:T(8,128)(2,1)}), bf16[16,256,1408]{1,0,2:T(8,128)(2,1)}, u32[]{:S(2)}, u32[]{:S(2)}) async-start(bf16[16,256,1408]{1,0,2:T(8,128)(2,1)} %divide_convert_fusion.1), calls=%async_computation | async-start | bytes 23068672 | tf_op jit(solution)/shard_map/all_to_all | solution.py:25
  242.8 132.7 %copy-start.3 = (f32[256,16]{0,1:T(8,128)S(1)}, f32[256,16]{0,1:T(8,128)}, u32[]{:S(2)}) copy-start(f32[256,16]{0,1:T(8,128)} %param.8) | copy-start | bytes 49156
  242.8 132.7 %copy-start.4 = (f32[256]{0:T(256)S(1)}, f32[256]{0:T(256)}, u32[]{:S(2)}) copy-start(f32[256]{0:T(256)} %param.9) | copy-start | bytes 3076
  370.2 211.0 %all-to-all-start.2 = ((bf16[16,1408,256]{2,0,1:T(8,128)(2,1)}), bf16[16,1408,256]{2,0,1:T(8,128)(2,1)}, u32[]{:S(2)}, u32[]{:S(2)}) async-start(bf16[16,1408,256]{2,0,1:T(8,128)(2,1)} %fusion), calls=%async_computation.2 | async-start | bytes 23068672 | tf_op jit(solution)/shard_map/all_to_all | solution.py:28
Sparse Core Ops, SparseCore 0:
  32.6 56.1 all-reduce.2
where the time goes:
time: 621 us; the launch traced here: 618 us
  waiting for transfers between devices  217 us (35%)
  local copies, waits for them, and re-layouts  145 us (23%)
  blocking collectives  145 us (23%)
  other arithmetic  81.3 us (13%)
  starting transfers between devices  15.8 us (3%)
  between operations  14.2 us (2%)
    all_gather x1, blocking collectives, body(): row_router = lax.all_gather(part_router, 'fsdp', axis=0, tiled=True)  131 us
    all_to_all x1, waiting for transfers between devices, body(): lax.all_to_all(narrow_gate, 'fsdp', split_axis=2, concat_axis=1, tiled=True)  94.8 us
    all_to_all x1, waiting for transfers between devices, body(): lax.all_to_all(narrow_up, 'fsdp', split_axis=2, concat_axis=1, tiled=True)  89.5 us
    unnamed x13, local copies, waits for them, and re-layouts  53.2 us
    psum x1, waiting for transfers between devices, body(): lax.psum((jnp.sum(train_gate * train_gate, axis=1), jnp.sum(train_up * tr...  32.6 us
    convert_element_type x1, other arithmetic, body(): (train_down / jnp.expand_dims(scale_down, 2)).astype(jnp.bfloat16)  32.6 us
    all_to_all x2, local copies, waits for them, and re-layouts, body(): lax.all_to_all(narrow_up, 'fsdp', split_axis=2, concat_axis=1, tiled=True)  29.3 us
    all_to_all x2, local copies, waits for them, and re-layouts, body(): lax.all_to_all(narrow_gate, 'fsdp', split_axis=2, concat_axis=1, tiled=True)  29.3 us
  transfers between devices with their start and end apart: 4, of which 3 were waited for; matrix products, arithmetic and copies ran while one was open for 19% of the time, Pallas kernels for 0%

commit v1 on v0

v1 whole, which is shorter than its diff:
```python
import functools

import jax
import jax.numpy as jnp
from jax import lax
from jax.experimental import pallas as pl
from jax.experimental.pallas import tpu as pltpu
from jax.sharding import PartitionSpec as P

MESH = pl.DeviceIdType.MESH
VMEM = pltpu.VMEM


def bits_of(n):
    return n.bit_length() - 1


def plain_body(train_gate, train_up, train_down, router_weight, router_gain):
    total_gate, total_up, total_down = lax.psum(
        (
            jnp.sum(train_gate * train_gate, axis=1),
            jnp.sum(train_up * train_up, axis=1),
            jnp.sum(train_down * train_down, axis=2),
        ),
        "fsdp",
    )
    scale_gate = jnp.sqrt(total_gate)
    scale_up = jnp.sqrt(total_up)
    scale_down = jnp.sqrt(total_down)
    narrow_gate, narrow_up, narrow_down = (
        (train_gate / jnp.expand_dims(scale_gate, 1)).astype(jnp.bfloat16),
        (train_up / jnp.expand_dims(scale_up, 1)).astype(jnp.bfloat16),
        (train_down / jnp.expand_dims(scale_down, 2)).astype(jnp.bfloat16),
    )
    ready_gate = lax.all_to_all(narrow_gate, "fsdp", split_axis=2, concat_axis=1, tiled=True)
    ready_up = lax.all_to_all(narrow_up, "fsdp", split_axis=2, concat_axis=1, tiled=True)
    ready_down = lax.all_to_all(narrow_down, "fsdp", split_axis=1, concat_axis=2, tiled=True)
    piece = ready_gate.shape[2]
    mine = lambda s: lax.dynamic_slice_in_dim(s, lax.axis_index("fsdp") * piece, piece, axis=1)
    part_router = (router_weight * router_gain[:, None]).astype(jnp.bfloat16)
    row_router = lax.all_gather(part_router, "fsdp", axis=0, tiled=True)
    serve_router = lax.all_gather(row_router, "ep", axis=1, tiled=True)
    return (ready_gate, ready_up, ready_down, mine(scale_gate), mine(scale_up), mine(scale_down), serve_router)


def column_of(row, width):
    return jnp.broadcast_to(row, (width, row.shape[1])).T


def sums_kernel(gate_ref, up_ref, down_ref, gate_out, up_out, down_out):
    e = pl.program_id(0)
    g, u, d = gate_ref[0], up_ref[0], down_ref[0]
    gate_out[pl.ds(e, 1), :] = jnp.sum(g * g, axis=0, keepdims=True)
    up_out[pl.ds(e, 1), :] = jnp.sum(u * u, axis=0, keepdims=True)
    d = d * d
    folded = d[:, :128]
    for at in range(128, d.shape[1], 128):
        folded = folded + d[:, at : at + 128]
    down_out[pl.ds(e, 1), :] = jnp.sum(folded.T, axis=0, keepdims=True)


def sums(gate, up, down):
    experts, rows, wide = gate.shape
    out = jax.ShapeDtypeStruct((experts, wide), jnp.float32)
    whole = pl.BlockSpec((experts, wide), lambda e: (0, 0))
    return pl.pallas_call(
        sums_kernel,
        grid=(experts,),
        out_shape=(out, out, out),
        in_specs=[
            pl.BlockSpec((1, rows, wide), lambda e: (e, 0, 0)),
            pl.BlockSpec((1, rows, wide), lambda e: (e, 0, 0)),
            pl.BlockSpec((1, wide, rows), lambda e: (e, 0, 0)),
        ],
        out_specs=(whole, whole, whole),
        cost_estimate=pl.CostEstimate(flops=6 * gate.size, bytes_accessed=12 * gate.size, transcendentals=0),
        name="sums",
    )(gate, up, down)


def share_kernel(n_ep, n_fsdp, part_ref, router_ref, scale_ref, all_ref, total, landed, send, recv, rsend, rrecv):
    ep, me = lax.axis_index("ep"), lax.axis_index("fsdp")
    eb, fb = bits_of(n_ep), bits_of(n_fsdp)

    def flip(i, b):
        return i + (1 << b) - 2 * (1 << b) * ((i // (1 << b)) % 2)

    ep_peers = [(flip(ep, b), me) for b in range(eb)]
    fsdp_peers = [(ep, flip(me, b)) for b in range(fb)]
    barrier = pltpu.get_barrier_semaphore()
    for peer in ep_peers + fsdp_peers:
        pl.semaphore_signal(barrier, inc=1, device_id=peer, device_id_type=MESH)

    all_ref[ep, me] = router_ref[...]
    pl.semaphore_wait(barrier, eb + fb)

    half = total.shape[0]
    core = me % 2
    keep = pl.multiple_of(core * half, 8)
    give = pl.multiple_of((1 - core) * half, 8)

    def sum_copy(k):
        if k == 0:
            src, dst, peer = part_ref.at[pl.ds(give, half), :], landed.at[0], fsdp_peers[0]
        elif k < fb:
            src, dst, peer = total, landed.at[k], fsdp_peers[k]
        else:
            src, dst, peer = scale_ref.at[pl.ds(keep, half), :], scale_ref.at[pl.ds(keep, half), :], fsdp_peers[0]
        return pltpu.make_async_remote_copy(src, dst, send.at[k], recv.at[k], device_id=peer, device_id_type=MESH)

    def router_copy(k):
        if k < eb:
            width = 1 << k
            block = all_ref.at[pl.ds(ep // width * width, width), pl.ds(me, 1)]
            peer = ep_peers[k]
        else:
            width = 1 << (k - eb)
            block = all_ref.at[:, pl.ds(me // width * width, width)]
            peer = fsdp_peers[k - eb]
        return pltpu.make_async_remote_copy(block, block, rsend.at[k], rrecv.at[k], device_id=peer, device_id_type=MESH)

    for k in range(max(fb + 1, eb + fb)):
        if k <= fb:
            sc = sum_copy(k)
            sc.start()
        if k < eb + fb:
            rc = router_copy(k)
            rc.start()
        if k <= fb:
            sc.wait()
            if k == 0:
                total[...] = part_ref[pl.ds(keep, half), :] + landed[0]
            elif k < fb:
                total[...] = total[...] + landed[k]
            if k == fb - 1:
                scale_ref[pl.ds(keep, half), :] = jnp.sqrt(total[...])
        if k < eb + fb:
            rc.wait()


def share(mesh, part, router):
    n_ep, n_fsdp = mesh.shape["ep"], mesh.shape["fsdp"]
    rows, wide = part.shape
    eb, fb = bits_of(n_ep), bits_of(n_fsdp)
    vmem = pl.BlockSpec(memory_space=VMEM)
    dma = pltpu.SemaphoreType.DMA
    return pl.pallas_call(
        functools.partial(share_kernel, n_ep, n_fsdp),
        out_shape=(
            jax.ShapeDtypeStruct(part.shape, jnp.float32),
            jax.ShapeDtypeStruct((n_ep, n_fsdp) + router.shape, router.dtype),
        ),
        in_specs=[vmem, vmem],
        out_specs=(vmem, vmem),
        scratch_shapes=[
            VMEM((rows // 2, wide), jnp.float32),
            VMEM((fb, rows // 2, wide), jnp.float32),
            dma((fb + 1,)),
            dma((fb + 1,)),
            dma((eb + fb,)),
            dma((eb + fb,)),
        ],
        compiler_params=pltpu.CompilerParams(collective_id=0, has_side_effects=True),
        cost_estimate=pl.CostEstimate(flops=part.size, bytes_accessed=32 << 20, transcendentals=0),
        name="share",
    )(part, router)


def pack_kernel(turned, offset, x_ref, scale_ref, out_ref):
    e = pl.program_id(0)
    inverse = 1.0 / scale_ref[pl.ds(e + offset, 1), :]
    pieces, piece = out_ref.shape[0], out_ref.shape[2]
    if turned:
        y = (x_ref[0] * inverse).astype(jnp.bfloat16).T
        for j in range(pieces):
            out_ref[j, 0] = y[j * piece : (j + 1) * piece, :]
    else:
        column = column_of(inverse, 128)
        for at in range(0, x_ref.shape[2], 128):
            y = (x_ref[0, :, at : at + 128] * column).astype(jnp.bfloat16)
            for j in range(pieces):
                out_ref[j, 0, :, at : at + 128] = y[j * piece : (j + 1) * piece, :]


def pack(x, scale, pieces, turned, offset, name):
    experts = x.shape[0]
    rows, wide = (x.shape[1], x.shape[2]) if turned else (x.shape[2], x.shape[1])
    piece = wide // pieces
    return pl.pallas_call(
        functools.partial(pack_kernel, turned, offset),
        grid=(experts,),
        out_shape=jax.ShapeDtypeStruct((pieces, experts, piece, rows), jnp.bfloat16),
        in_specs=[
            pl.BlockSpec((1,) + x.shape[1:], lambda e: (e, 0, 0)),
            pl.BlockSpec(scale.shape, lambda e: (0, 0)),
        ],
        out_specs=pl.BlockSpec((pieces, 1, piece, rows), lambda e: (0, e, 0, 0)),
        cost_estimate=pl.CostEstimate(flops=2 * x.size, bytes_accessed=6 * x.size, transcendentals=0),
        name=name,
    )(x, scale)


def place_kernel(in_ref, out_ref):
    pieces, rows = in_ref.shape[0], in_ref.shape[3]
    for s in range(pieces):
        out_ref[0, :, s * rows : (s + 1) * rows] = in_ref[s, 0]


def place(x, name):
    pieces, experts, piece, rows = x.shape
    shape = (piece, pieces * rows)
    return pl.pallas_call(
        place_kernel,
        grid=(experts,),
        out_shape=jax.ShapeDtypeStruct((experts,) + shape, x.dtype),
        in_specs=[pl.BlockSpec((pieces, 1, piece, rows), lambda e: (0, e, 0, 0))],
        out_specs=pl.BlockSpec((1,) + shape, lambda e: (e, 0, 0)),
        cost_estimate=pl.CostEstimate(flops=x.size, bytes_accessed=4 * x.size, transcendentals=0),
        name=name,
    )(x)


def body(mesh, train_gate, train_up, train_down, router_weight, router_gain):
    n = mesh.shape["fsdp"]
    experts, rows, wide = train_gate.shape
    piece = wide // n
    parts = sums(train_gate, train_up, train_down)
    router = (router_weight.T * router_gain[None, :]).astype(jnp.bfloat16)
    scale, gathered = share(mesh, jnp.concatenate(parts, axis=0), router)

    swap = lambda x: lax.all_to_all(x, "fsdp", split_axis=0, concat_axis=0, tiled=True)
    sent_gate = pack(train_gate, scale, n, True, 0, "pack_gate")
    got_gate = swap(sent_gate)
    sent_up = pack(train_up, scale, n, True, experts, "pack_up")
    got_up = swap(sent_up)
    sent_down = pack(train_down, scale, n, False, 2 * experts, "pack_down")
    got_down = swap(sent_down)
    ready_gate = place(got_gate, "place_gate").swapaxes(1, 2)
    ready_up = place(got_up, "place_up").swapaxes(1, 2)
    ready_down = place(got_down, "place_down")

    mine = lax.dynamic_slice_in_dim(scale, lax.axis_index("fsdp") * piece, piece, axis=1)
    serve_router = gathered.transpose(0, 2, 1, 3).reshape(-1, n * rows).T
    return (
        ready_gate,
        ready_up,
        ready_down,
        mine[:experts],
        mine[experts : 2 * experts],
        mine[2 * experts :],
        serve_router,
    )


def solution(mesh):
    def step(gate, up, down, weight, gain):
        n_ep, n = mesh.shape["ep"], mesh.shape["fsdp"]
        experts, rows, wide = gate.shape
        powers = n & (n - 1) == 0 and n_ep & (n_ep - 1) == 0 and n > 1
        if powers and rows % 128 == 0 and wide % (16 * n) == 0 and wide % 128 == 0 and experts % 16 == 0:
            return body(mesh, gate, up, down, weight, gain)
        return plain_body(gate, up, down, weight, gain)

    return jax.shard_map(
        step,
        mesh=mesh,
        in_specs=(
            P("ep", "fsdp", None),
            P("ep", "fsdp", None),
            P("ep", None, "fsdp"),
            P("fsdp", "ep"),
            P("fsdp"),
        ),
        out_specs=(
            P("ep", None, "fsdp"),
            P("ep", None, "fsdp"),
            P("ep", "fsdp", None),
            P("ep", "fsdp"),
            P("ep", "fsdp"),
            P("ep", "fsdp"),
            P(),
        ),
        check_vma=False,
    )
```

time: 621 us -> 487 us (0.78)
  Pallas kernels: 0 us -> 149 us
  blocking collectives: 145 us -> 0 us
  local copies, waits for them, and re-layouts: 145 us -> 2.32 us
  waiting for transfers between devices: 217 us -> 315 us
  other arithmetic: 81.3 us -> 2.3 us
  between operations: 14.2 us -> 0.71 us
    pallas_call x0 -> x8, Pallas kernels: none -> 149 us  [the longest x3 55.2 us: pack(): pl.pallas_call(functools.partial(pack_kernel, turned, offset), grid=(expe...]
    all_gather x2 -> x0, blocking collectives: 145 us -> none  [the longest x1 131 us: body(): row_router = lax.all_gather(part_router, 'fsdp', axis=0, tiled=True)]
    all_to_all x3, waiting for transfers between devices: 184 us -> 315 us  [body(): lax.all_to_all(x, 'fsdp', split_axis=0, concat_axis=0, tiled=True)]
    all_to_all x6 -> x0, local copies, waits for them, and re-layouts: 87.9 us -> none  [the longest x2 29.3 us: body(): lax.all_to_all(narrow_up, 'fsdp', split_axis=2, concat_axis=1, tiled=True)]
    convert_element_type x4 -> x1, other arithmetic: 61.1 us -> 0.6 us  [body(): router = (router_weight.T * router_gain[None, :]).astype(jnp.bfloat16)]
    unnamed x13 -> x7, local copies, waits for them, and re-layouts: 53.2 us -> 0.77 us
    psum x1 -> x0, waiting for transfers between devices: 32.6 us -> none  [body(): lax.psum((jnp.sum(train_gate * train_gate, axis=1), jnp.sum(train_up * tr...]
    reduce_sum x2 -> x0, other arithmetic: 20.2 us -> none  [the longest x1 11 us: body(): jnp.sum(train_up * train_up, axis=1)]
  transfers between devices with their start and end apart: 4 -> 3, of which waited for: 3 -> 3; matrix products, arithmetic and copies ran while one was open for 19% -> 0% of each run, Pallas kernels for 0% -> 14%
where the time goes in v1:
time: 487 us; the launch traced here: 485 us
  waiting for transfers between devices  315 us (65%)
  Pallas kernels  149 us (31%)
  starting transfers between devices  15.8 us (3%)
    all_to_all x3, waiting for transfers between devices, body(): lax.all_to_all(x, 'fsdp', split_axis=0, concat_axis=0, tiled=True)  315 us
    pallas_call x3, Pallas kernels, pack(): pl.pallas_call(functools.partial(pack_kernel, turned, offset), grid=(expe...  55.2 us
    pallas_call x3, Pallas kernels, place(): pl.pallas_call(place_kernel, grid=(experts,), out_shape=jax.ShapeDtypeStr...  44.3 us
    pallas_call x1, Pallas kernels, sums(): pl.pallas_call(sums_kernel, grid=(experts,), out_shape=(out, out, out), i...  24.9 us
    pallas_call x1, Pallas kernels, share(): pl.pallas_call(functools.partial(share_kernel, n_ep, n_fsdp), out_shape=(...  24.5 us
    all_to_all x3, starting transfers between devices, body(): lax.all_to_all(x, 'fsdp', split_axis=0, concat_axis=0, tiled=True)  15.8 us
  transfers between devices with their start and end apart: 3, of which 3 were waited for; matrix products, arithmetic and copies ran while one was open for 0% of the time, Pallas kernels for 14%

profile of v1, /device:TPU:0, one launch (start us, length us, event | category | flops | bytes accessed | tf_op | source)
XLA Modules:
  0.0 484.7 jit_solution(12487982815567984640)
XLA Ops:
  0.6 0.0 copy-start.2
  0.6 0.0 copy-start.1
  0.7 24.9 %sums.1 = (f32[16,1408]{1,0:T(8,128)}, f32[16,1408]{1,0:T(8,128)}, f32[16,1408]{1,0:T(8,128)}) custom-call(f32[16,256,1408]{2,1,0:T(8,128)} %x_ref.3, f32[16,256,1408]{2,1,0:T(8,128)} %x_ref.4, f32[16,1408,256]{2,1,0:T(8,128)} %x_ref.5), custom_call_target="tpu_custom_call" | custom-call | flops 34603008 | bytes 69206016 | tf_op jit(solution)/shard_map/sums/pallas_call | solution.py:66
  25.5 1.7 pad_maximum_fusion.part_ref
  27.2 0.0 copy-done.2
  27.2 0.0 copy-done.1
  27.2 0.6 fusion.router_ref
  27.8 24.5 %share.1 = (f32[48,1408]{1,0:T(8,128)}, bf16[4,8,16,256]{3,2,1,0:T(8,128)(2,1)}) custom-call(f32[48,1408]{1,0:T(8,128)} %pad_maximum_fusion.part_ref, bf16[16,256]{1,0:T(8,128)(2,1)} %fusion.router_ref), custom_call_target="tpu_custom_call" | custom-call | flops 67584 | bytes 33554432 | tf_op jit(solution)/shard_map/share/pallas_call | solution.py:147
  52.3 18.5 %pack_down.1 = bf16[8,16,176,256]{3,2,1,0:T(8,128)(2,1)} custom-call(f32[16,1408,256]{2,1,0:T(8,128)} %x_ref.5, f32[48,1408]{1,0:T(8,128)} %get-tuple-element.15.scale_ref), custom_call_target="tpu_custom_call" | custom-call | flops 11534336 | bytes 34603008 | tf_op jit(solution)/shard_map/pack_down/pallas_call | solution.py:189
  70.9 5.2 %all-to-all-start.2 = ((bf16[8,16,176,256]{3,2,1,0:T(8,128)(2,1)}), bf16[8,16,176,256]{3,2,1,0:T(8,128)(2,1)}, u32[]{:S(2)}, u32[]{:S(2)}) async-start(bf16[8,16,176,256]{3,2,1,0:T(8,128)(2,1)} %pack_down.1), calls=%async_computation.2 | async-start | bytes 23068672 | tf_op jit(solution)/shard_map/all_to_all | solution.py:231
  76.1 18.3 %pack_up.1 = bf16[8,16,176,256]{3,2,1,0:T(8,128)(2,1)} custom-call(f32[16,256,1408]{2,1,0:T(8,128)} %x_ref.4, f32[48,1408]{1,0:T(8,128)} %get-tuple-element.15.scale_ref), custom_call_target="tpu_custom_call" | custom-call | flops 11534336 | bytes 34603008 | tf_op jit(solution)/shard_map/pack_up/pallas_call | solution.py:189
  94.5 109.4 %all-to-all-done.2.in_ref = bf16[8,16,176,256]{3,2,1,0:T(8,128)(2,1)} async-done(((bf16[8,16,176,256]{3,2,1,0:T(8,128)(2,1)}), bf16[8,16,176,256]{3,2,1,0:T(8,128)(2,1)}, u32[]{:S(2)}, u32[]{:S(2)}) %all-to-all-start.2) | async-done | bytes 11534368 | tf_op jit(solution)/shard_map/all_to_all | solution.py:231
  203.9 5.3 %all-to-all-start.1 = ((bf16[8,16,176,256]{3,2,1,0:T(8,128)(2,1)}), bf16[8,16,176,256]{3,2,1,0:T(8,128)(2,1)}, u32[]{:S(2)}, u32[]{:S(2)}) async-start(bf16[8,16,176,256]{3,2,1,0:T(8,128)(2,1)} %pack_up.1), calls=%async_computation.1 | async-start | bytes 23068672 | tf_op jit(solution)/shard_map/all_to_all | solution.py:231
  209.2 18.3 %pack_gate.1 = bf16[8,16,176,256]{3,2,1,0:T(8,128)(2,1)} custom-call(f32[16,256,1408]{2,1,0:T(8,128)} %x_ref.3, f32[48,1408]{1,0:T(8,128)} %get-tuple-element.15.scale_ref), custom_call_target="tpu_custom_call" | custom-call | flops 11534336 | bytes 34603008 | tf_op jit(solution)/shard_map/pack_gate/pallas_call | solution.py:189
  227.5 109.4 %all-to-all-done.1.in_ref = bf16[8,16,176,256]{3,2,1,0:T(8,128)(2,1)} async-done(((bf16[8,16,176,256]{3,2,1,0:T(8,128)(2,1)}), bf16[8,16,176,256]{3,2,1,0:T(8,128)(2,1)}, u32[]{:S(2)}, u32[]{:S(2)}) %all-to-all-start.1) | async-done | bytes 11534368 | tf_op jit(solution)/shard_map/all_to_all | solution.py:231
  336.9 5.3 %all-to-all-start = ((bf16[8,16,176,256]{3,2,1,0:T(8,128)(2,1)}), bf16[8,16,176,256]{3,2,1,0:T(8,128)(2,1)}, u32[]{:S(2)}, u32[]{:S(2)}) async-start(bf16[8,16,176,256]{3,2,1,0:T(8,128)(2,1)} %pack_gate.1), calls=%async_computation | async-start | bytes 23068672 | tf_op jit(solution)/shard_map/all_to_all | solution.py:231
  342.2 0.0 copy-done
  342.2 0.1 copy.12
  342.3 0.8 copy.13
  343.0 1.5 fusion.1
  344.5 14.8 %place_down.1 = bf16[16,176,2048]{2,1,0:T(8,128)(2,1)} custom-call(bf16[8,16,176,256]{3,2,1,0:T(8,128)(2,1)} %all-to-all-done.2.in_ref), custom_call_target="tpu_custom_call" | custom-call | flops 5767168 | bytes 23068672 | tf_op jit(solution)/shard_map/place_down/pallas_call | solution.py:212
  359.3 14.8 %place_up.1 = bf16[16,176,2048]{2,1,0:T(8,128)(2,1)} custom-call(bf16[8,16,176,256]{3,2,1,0:T(8,128)(2,1)} %all-to-all-done.1.in_ref), custom_call_target="tpu_custom_call" | custom-call | flops 5767168 | bytes 23068672 | tf_op jit(solution)/shard_map/place_up/pallas_call | solution.py:212
  374.0 95.9 %all-to-all-done.in_ref = bf16[8,16,176,256]{3,2,1,0:T(8,128)(2,1)} async-done(((bf16[8,16,176,256]{3,2,1,0:T(8,128)(2,1)}), bf16[8,16,176,256]{3,2,1,0:T(8,128)(2,1)}, u32[]{:S(2)}, u32[]{:S(2)}) %all-to-all-start) | async-done | bytes 11534368 | tf_op jit(solution)/shard_map/all_to_all | solution.py:231
  469.9 14.8 %place_gate.1 = bf16[16,176,2048]{2,1,0:T(8,128)(2,1)} custom-call(bf16[8,16,176,256]{3,2,1,0:T(8,128)(2,1)} %all-to-all-done.in_ref), custom_call_target="tpu_custom_call" | custom-call | flops 5767168 | bytes 23068672 | tf_op jit(solution)/shard_map/place_gate/pallas_call | solution.py:212
  (1 shorter events, 0.0 us)
Async XLA Ops:
  0.6 26.6 %copy-start.2 = (f32[256]{0:T(256)S(1)}, f32[256]{0:T(256)}, u32[]{:S(2)}) copy-start(f32[256]{0:T(256)} %param.9) | copy-start | bytes 3076
  0.6 26.6 %copy-start.1 = (f32[256,16]{0,1:T(8,128)S(1)}, f32[256,16]{0,1:T(8,128)}, u32[]{:S(2)}) copy-start(f32[256,16]{0,1:T(8,128)} %param.8) | copy-start | bytes 49156
  70.9 133.0 %all-to-all-start.2 = ((bf16[8,16,176,256]{3,2,1,0:T(8,128)(2,1)}), bf16[8,16,176,256]{3,2,1,0:T(8,128)(2,1)}, u32[]{:S(2)}, u32[]{:S(2)}) async-start(bf16[8,16,176,256]{3,2,1,0:T(8,128)(2,1)} %pack_down.1), calls=%async_computation.2 | async-start | bytes 23068672 | tf_op jit(solution)/shard_map/all_to_all | solution.py:231
  203.9 133.1 %all-to-all-start.1 = ((bf16[8,16,176,256]{3,2,1,0:T(8,128)(2,1)}), bf16[8,16,176,256]{3,2,1,0:T(8,128)(2,1)}, u32[]{:S(2)}, u32[]{:S(2)}) async-start(bf16[8,16,176,256]{3,2,1,0:T(8,128)(2,1)} %pack_up.1), calls=%async_computation.1 | async-start | bytes 23068672 | tf_op jit(solution)/shard_map/all_to_all | solution.py:231
  227.5 114.7 %copy-start = (bf16[4,8,16,256]{3,2,1,0:T(8,128)(2,1)S(1)}, bf16[4,8,16,256]{3,2,1,0:T(8,128)(2,1)}, u32[]{:S(2)}) copy-start(bf16[4,8,16,256]{3,2,1,0:T(8,128)(2,1)} %get-tuple-element.16) | copy-start | bytes 786436
  336.9 133.0 %all-to-all-start = ((bf16[8,16,176,256]{3,2,1,0:T(8,128)(2,1)}), bf16[8,16,176,256]{3,2,1,0:T(8,128)(2,1)}, u32[]{:S(2)}, u32[]{:S(2)}) async-start(bf16[8,16,176,256]{3,2,1,0:T(8,128)(2,1)} %pack_gate.1), calls=%async_computation | async-start | bytes 23068672 | tf_op jit(solution)/shard_map/all_to_all | solution.py:231

commit v2 on v1

--- a/solution.py
+++ b/solution.py
@@ -47,32 +47,31 @@
     return jnp.broadcast_to(row, (width, row.shape[1])).T
 
 
-def sums_kernel(gate_ref, up_ref, down_ref, gate_out, up_out, down_out):
-    e = pl.program_id(0)
-    g, u, d = gate_ref[0], up_ref[0], down_ref[0]
-    gate_out[pl.ds(e, 1), :] = jnp.sum(g * g, axis=0, keepdims=True)
-    up_out[pl.ds(e, 1), :] = jnp.sum(u * u, axis=0, keepdims=True)
-    d = d * d
-    folded = d[:, :128]
-    for at in range(128, d.shape[1], 128):
-        folded = folded + d[:, at : at + 128]
-    down_out[pl.ds(e, 1), :] = jnp.sum(folded.T, axis=0, keepdims=True)
-
-
-def sums(gate, up, down):
+def sums_kernel(experts, block, gate_ref, up_ref, down_ref, out_ref):
+    for i in range(block):
+        e = pl.program_id(0) * block + i
+        g, u, d = gate_ref[i], up_ref[i], down_ref[i]
+        out_ref[pl.ds(e, 1), :] = jnp.sum(g * g, axis=0, keepdims=True)
+        out_ref[pl.ds(e + experts, 1), :] = jnp.sum(u * u, axis=0, keepdims=True)
+        d = d * d
+        folded = d[:, :128]
+        for at in range(128, d.shape[1], 128):
+            folded = folded + d[:, at : at + 128]
+        out_ref[pl.ds(e + 2 * experts, 1), :] = jnp.sum(folded.T, axis=0, keepdims=True)
+
+
+def sums(gate, up, down, block=2):
     experts, rows, wide = gate.shape
-    out = jax.ShapeDtypeStruct((experts, wide), jnp.float32)
-    whole = pl.BlockSpec((experts, wide), lambda e: (0, 0))
-    return pl.pallas_call(
-        sums_kernel,
-        grid=(experts,),
-        out_shape=(out, out, out),
+    return pl.pallas_call(
+        functools.partial(sums_kernel, experts, block),
+        grid=(experts // block,),
+        out_shape=jax.ShapeDtypeStruct((3 * experts, wide), jnp.float32),
         in_specs=[
-            pl.BlockSpec((1, rows, wide), lambda e: (e, 0, 0)),
-            pl.BlockSpec((1, rows, wide), lambda e: (e, 0, 0)),
-            pl.BlockSpec((1, wide, rows), lambda e: (e, 0, 0)),
+            pl.BlockSpec((block, rows, wide), lambda e: (e, 0, 0)),
+            pl.BlockSpec((block, rows, wide), lambda e: (e, 0, 0)),
+            pl.BlockSpec((block, wide, rows), lambda e: (e, 0, 0)),
         ],
-        out_specs=(whole, whole, whole),
+        out_specs=pl.BlockSpec((3 * experts, wide), lambda e: (0, 0)),
         cost_estimate=pl.CostEstimate(flops=6 * gate.size, bytes_accessed=12 * gate.size, transcendentals=0),
         name="sums",
     )(gate, up, down)
@@ -80,22 +79,26 @@
 
 def share_kernel(n_ep, n_fsdp, part_ref, router_ref, scale_ref, all_ref, total, landed, send, recv, rsend, rrecv):
     ep, me = lax.axis_index("ep"), lax.axis_index("fsdp")
-    eb, fb = bits_of(n_ep), bits_of(n_fsdp)
-
-    def flip(i, b):
-        return i + (1 << b) - 2 * (1 << b) * ((i // (1 << b)) % 2)
-
-    ep_peers = [(flip(ep, b), me) for b in range(eb)]
-    fsdp_peers = [(ep, flip(me, b)) for b in range(fb)]
+    fb = bits_of(n_fsdp)
+
+    core = me % 2
+
+    def flip(i, w):
+        return i + w - 2 * w * ((i // w) % 2)
+
+    ep_peers = [((ep + d) % n_ep, me) for d in range(1, n_ep)]
+    fsdp_peers = [(ep, flip(me, 1 << b)) for b in range(fb)]
+    sum_peers = fsdp_peers[:1] + [
+        (ep, flip(me, (1 << k) * (1 - core) + (1 << (fb - k)) * core)) for k in range(1, fb)
+    ]
     barrier = pltpu.get_barrier_semaphore()
     for peer in ep_peers + fsdp_peers:
         pl.semaphore_signal(barrier, inc=1, device_id=peer, device_id_type=MESH)
 
     all_ref[ep, me] = router_ref[...]
-    pl.semaphore_wait(barrier, eb + fb)
+    pl.semaphore_wait(barrier, n_ep - 1 + fb)
 
     half = total.shape[0]
-    core = me % 2
     keep = pl.multiple_of(core * half, 8)
     give = pl.multiple_of((1 - core) * half, 8)
 
@@ -103,45 +106,45 @@
         if k == 0:
             src, dst, peer = part_ref.at[pl.ds(give, half), :], landed.at[0], fsdp_peers[0]
         elif k < fb:
-            src, dst, peer = total, landed.at[k], fsdp_peers[k]
+            src, dst, peer = total, landed.at[k], sum_peers[k]
         else:
             src, dst, peer = scale_ref.at[pl.ds(keep, half), :], scale_ref.at[pl.ds(keep, half), :], fsdp_peers[0]
         return pltpu.make_async_remote_copy(src, dst, send.at[k], recv.at[k], device_id=peer, device_id_type=MESH)
 
-    def router_copy(k):
-        if k < eb:
-            width = 1 << k
-            block = all_ref.at[pl.ds(ep // width * width, width), pl.ds(me, 1)]
-            peer = ep_peers[k]
+    def router_copies(k):
+        if k == 0:
+            block = all_ref.at[ep, pl.ds(me, 1)]
+            pairs = [(d, ep_peers[d]) for d in range(n_ep - 1)]
         else:
-            width = 1 << (k - eb)
+            width = 1 << (k - 1)
             block = all_ref.at[:, pl.ds(me // width * width, width)]
-            peer = fsdp_peers[k - eb]
-        return pltpu.make_async_remote_copy(block, block, rsend.at[k], rrecv.at[k], device_id=peer, device_id_type=MESH)
-
-    for k in range(max(fb + 1, eb + fb)):
-        if k <= fb:
-            sc = sum_copy(k)
-            sc.start()
-        if k < eb + fb:
-            rc = router_copy(k)
+            pairs = [(n_ep - 2 + k, fsdp_peers[k - 1])]
+        return [
+            pltpu.make_async_remote_copy(block, block, rsend.at[i], rrecv.at[i], device_id=peer, device_id_type=MESH)
+            for i, peer in pairs
+        ]
+
+    for k in range(fb + 1):
+        sc = sum_copy(k)
+        sc.start()
+        rcs = router_copies(k)
+        for rc in rcs:
             rc.start()
-        if k <= fb:
-            sc.wait()
-            if k == 0:
-                total[...] = part_ref[pl.ds(keep, half), :] + landed[0]
-            elif k < fb:
-                total[...] = total[...] + landed[k]
-            if k == fb - 1:
-                scale_ref[pl.ds(keep, half), :] = jnp.sqrt(total[...])
-        if k < eb + fb:
+        sc.wait()
+        if k == 0:
+            total[...] = part_ref[pl.ds(keep, half), :] + landed[0]
+        elif k < fb:
+            total[...] = total[...] + landed[k]
+        if k == fb - 1:
+            scale_ref[pl.ds(keep, half), :] = jnp.sqrt(total[...])
+        for rc in rcs:
             rc.wait()
 
 
 def share(mesh, part, router):
     n_ep, n_fsdp = mesh.shape["ep"], mesh.shape["fsdp"]
     rows, wide = part.shape
-    eb, fb = bits_of(n_ep), bits_of(n_fsdp)
+    fb = bits_of(n_fsdp)
     vmem = pl.BlockSpec(memory_space=VMEM)
     dma = pltpu.SemaphoreType.DMA
     return pl.pallas_call(
@@ -157,8 +160,8 @@
             VMEM((fb, rows // 2, wide), jnp.float32),
             dma((fb + 1,)),
             dma((fb + 1,)),
-            dma((eb + fb,)),
-            dma((eb + fb,)),
+            dma((n_ep - 1 + fb,)),
+            dma((n_ep - 1 + fb,)),
         ],
         compiler_params=pltpu.CompilerParams(collective_id=0, has_side_effects=True),
         cost_estimate=pl.CostEstimate(flops=part.size, bytes_accessed=32 << 20, transcendentals=0),
@@ -166,55 +169,57 @@
     )(part, router)
 
 
-def pack_kernel(turned, offset, x_ref, scale_ref, out_ref):
-    e = pl.program_id(0)
-    inverse = 1.0 / scale_ref[pl.ds(e + offset, 1), :]
+def pack_kernel(turned, offset, block, x_ref, scale_ref, out_ref):
     pieces, piece = out_ref.shape[0], out_ref.shape[2]
-    if turned:
-        y = (x_ref[0] * inverse).astype(jnp.bfloat16).T
-        for j in range(pieces):
-            out_ref[j, 0] = y[j * piece : (j + 1) * piece, :]
-    else:
-        column = column_of(inverse, 128)
-        for at in range(0, x_ref.shape[2], 128):
-            y = (x_ref[0, :, at : at + 128] * column).astype(jnp.bfloat16)
+    for i in range(block):
+        e = pl.program_id(0) * block + i
+        inverse = 1.0 / scale_ref[pl.ds(e + offset, 1), :]
+        if turned:
+            y = (x_ref[i] * inverse).astype(jnp.bfloat16).T
             for j in range(pieces):
-                out_ref[j, 0, :, at : at + 128] = y[j * piece : (j + 1) * piece, :]
-
-
-def pack(x, scale, pieces, turned, offset, name):
+                out_ref[j, i] = y[j * piece : (j + 1) * piece, :]
+        else:
+            column = column_of(inverse, 128)
+            for at in range(0, x_ref.shape[2], 128):
+                y = (x_ref[i, :, at : at + 128] * column).astype(jnp.bfloat16)
+                for j in range(pieces):
+                    out_ref[j, i, :, at : at + 128] = y[j * piece : (j + 1) * piece, :]
+
+
+def pack(x, scale, pieces, turned, offset, name, block=2):
     experts = x.shape[0]
     rows, wide = (x.shape[1], x.shape[2]) if turned else (x.shape[2], x.shape[1])
     piece = wide // pieces
     return pl.pallas_call(
-        functools.partial(pack_kernel, turned, offset),
-        grid=(experts,),
+        functools.partial(pack_kernel, turned, offset, block),
+        grid=(experts // block,),
         out_shape=jax.ShapeDtypeStruct((pieces, experts, piece, rows), jnp.bfloat16),
         in_specs=[
-            pl.BlockSpec((1,) + x.shape[1:], lambda e: (e, 0, 0)),
+            pl.BlockSpec((block,) + x.shape[1:], lambda e: (e, 0, 0)),
             pl.BlockSpec(scale.shape, lambda e: (0, 0)),
         ],
-        out_specs=pl.BlockSpec((pieces, 1, piece, rows), lambda e: (0, e, 0, 0)),
+        out_specs=pl.BlockSpec((pieces, block, piece, rows), lambda e: (0, e, 0, 0)),
         cost_estimate=pl.CostEstimate(flops=2 * x.size, bytes_accessed=6 * x.size, transcendentals=0),
         name=name,
     )(x, scale)
 
 
 def place_kernel(in_ref, out_ref):
-    pieces, rows = in_ref.shape[0], in_ref.shape[3]
-    for s in range(pieces):
-        out_ref[0, :, s * rows : (s + 1) * rows] = in_ref[s, 0]
-
-
-def place(x, name):
+    pieces, block, _, rows = in_ref.shape
+    for i in range(block):
+        for s in range(pieces):
+            out_ref[i, :, s * rows : (s + 1) * rows] = in_ref[s, i]
+
+
+def place(x, name, block=4):
     pieces, experts, piece, rows = x.shape
     shape = (piece, pieces * rows)
     return pl.pallas_call(
         place_kernel,
-        grid=(experts,),
+        grid=(experts // block,),
         out_shape=jax.ShapeDtypeStruct((experts,) + shape, x.dtype),
-        in_specs=[pl.BlockSpec((pieces, 1, piece, rows), lambda e: (0, e, 0, 0))],
-        out_specs=pl.BlockSpec((1,) + shape, lambda e: (e, 0, 0)),
+        in_specs=[pl.BlockSpec((pieces, block, piece, rows), lambda e: (0, e, 0, 0))],
+        out_specs=pl.BlockSpec((block,) + shape, lambda e: (e, 0, 0)),
         cost_estimate=pl.CostEstimate(flops=x.size, bytes_accessed=4 * x.size, transcendentals=0),
         name=name,
     )(x)
@@ -226,7 +231,7 @@
     piece = wide // n
     parts = sums(train_gate, train_up, train_down)
     router = (router_weight.T * router_gain[None, :]).astype(jnp.bfloat16)
-    scale, gathered = share(mesh, jnp.concatenate(parts, axis=0), router)
+    scale, gathered = share(mesh, parts, router)
 
     swap = lambda x: lax.all_to_all(x, "fsdp", split_axis=0, concat_axis=0, tiled=True)
     sent_gate = pack(train_gate, scale, n, True, 0, "pack_gate")

time: 487 us -> 471 us (0.967)
  Pallas kernels: 149 us -> 116 us
  waiting for transfers between devices: 315 us -> 334 us
    pallas_call x7, Pallas kernels: 124 us -> 92.7 us  [the longest x3 43 us: pack(): pl.pallas_call(functools.partial(pack_kernel, turned, offset, block), gri...]
    all_to_all x3, waiting for transfers between devices: 315 us -> 334 us  [body(): lax.all_to_all(x, 'fsdp', split_axis=0, concat_axis=0, tiled=True)]
  transfers between devices with their start and end apart: 3 -> 3, of which waited for: 3 -> 3; matrix products, arithmetic and copies ran while one was open for 0% -> 0% of each run, Pallas kernels for 14% -> 10%
where the time goes in v2:
time: 471 us; the launch traced here: 470 us
  waiting for transfers between devices  334 us (71%)
  Pallas kernels  116 us (25%)
  starting transfers between devices  15.8 us (3%)
    all_to_all x3, waiting for transfers between devices, body(): lax.all_to_all(x, 'fsdp', split_axis=0, concat_axis=0, tiled=True)  334 us
    pallas_call x3, Pallas kernels, pack(): pl.pallas_call(functools.partial(pack_kernel, turned, offset, block), gri...  43 us
    pallas_call x3, Pallas kernels, place(): pl.pallas_call(place_kernel, grid=(experts // block,), out_shape=jax.Shap...  27.1 us
    pallas_call x1, Pallas kernels, share(): pl.pallas_call(functools.partial(share_kernel, n_ep, n_fsdp), out_shape=(...  23 us
    pallas_call x1, Pallas kernels, sums(): pl.pallas_call(functools.partial(sums_kernel, experts, block), grid=(expe...  22.6 us
    all_to_all x3, starting transfers between devices, body(): lax.all_to_all(x, 'fsdp', split_axis=0, concat_axis=0, tiled=True)  15.8 us
  transfers between devices with their start and end apart: 3, of which 3 were waited for; matrix products, arithmetic and copies ran while one was open for 0% of the time, Pallas kernels for 10%

profile of v2, /device:TPU:0, one launch (start us, length us, event | category | flops | bytes accessed | tf_op | source)
XLA Modules:
  0.0 470.1 jit_solution(15542053052722980756)
XLA Ops:
  0.6 1.3 fusion.router_ref
  2.0 22.6 %sums.1.part_ref = f32[48,1408]{1,0:T(8,128)} custom-call(f32[16,256,1408]{2,1,0:T(8,128)} %x_ref.3, f32[16,256,1408]{2,1,0:T(8,128)} %x_ref.4, f32[16,1408,256]{2,1,0:T(8,128)} %x_ref.5), custom_call_target="tpu_custom_call" | custom-call | flops 34603008 | bytes 69206016 | tf_op jit(solution)/shard_map/sums/pallas_call | solution.py:65
  24.6 23.0 %share.1 = (f32[48,1408]{1,0:T(8,128)}, bf16[4,8,16,256]{3,2,1,0:T(8,128)(2,1)}) custom-call(f32[48,1408]{1,0:T(8,128)} %sums.1.part_ref, bf16[16,256]{1,0:T(8,128)(2,1)} %fusion.router_ref), custom_call_target="tpu_custom_call" | custom-call | flops 67584 | bytes 33554432 | tf_op jit(solution)/shard_map/share/pallas_call | solution.py:150
  47.6 14.4 %pack_down.1 = bf16[8,16,176,256]{3,2,1,0:T(8,128)(2,1)} custom-call(f32[16,1408,256]{2,1,0:T(8,128)} %x_ref.5, f32[48,1408]{1,0:T(8,128)} %get-tuple-element.9.scale_ref), custom_call_target="tpu_custom_call" | custom-call | flops 11534336 | bytes 34603008 | tf_op jit(solution)/shard_map/pack_down/pallas_call | solution.py:193
  62.0 5.2 %all-to-all-start.2 = ((bf16[8,16,176,256]{3,2,1,0:T(8,128)(2,1)}), bf16[8,16,176,256]{3,2,1,0:T(8,128)(2,1)}, u32[]{:S(2)}, u32[]{:S(2)}) async-start(bf16[8,16,176,256]{3,2,1,0:T(8,128)(2,1)} %pack_down.1), calls=%async_computation.2 | async-start | bytes 23068672 | tf_op jit(solution)/shard_map/all_to_all | solution.py:236
  67.2 14.3 %pack_up.1 = bf16[8,16,176,256]{3,2,1,0:T(8,128)(2,1)} custom-call(f32[16,256,1408]{2,1,0:T(8,128)} %x_ref.4, f32[48,1408]{1,0:T(8,128)} %get-tuple-element.9.scale_ref), custom_call_target="tpu_custom_call" | custom-call | flops 11534336 | bytes 34603008 | tf_op jit(solution)/shard_map/pack_up/pallas_call | solution.py:193
  81.6 113.4 %all-to-all-done.2.in_ref = bf16[8,16,176,256]{3,2,1,0:T(8,128)(2,1)} async-done(((bf16[8,16,176,256]{3,2,1,0:T(8,128)(2,1)}), bf16[8,16,176,256]{3,2,1,0:T(8,128)(2,1)}, u32[]{:S(2)}, u32[]{:S(2)}) %all-to-all-start.2) | async-done | bytes 11534368 | tf_op jit(solution)/shard_map/all_to_all | solution.py:236
  195.0 5.3 %all-to-all-start.1 = ((bf16[8,16,176,256]{3,2,1,0:T(8,128)(2,1)}), bf16[8,16,176,256]{3,2,1,0:T(8,128)(2,1)}, u32[]{:S(2)}, u32[]{:S(2)}) async-start(bf16[8,16,176,256]{3,2,1,0:T(8,128)(2,1)} %pack_up.1), calls=%async_computation.1 | async-start | bytes 23068672 | tf_op jit(solution)/shard_map/all_to_all | solution.py:236
  200.3 14.3 %pack_gate.1 = bf16[8,16,176,256]{3,2,1,0:T(8,128)(2,1)} custom-call(f32[16,256,1408]{2,1,0:T(8,128)} %x_ref.3, f32[48,1408]{1,0:T(8,128)} %get-tuple-element.9.scale_ref), custom_call_target="tpu_custom_call" | custom-call | flops 11534336 | bytes 34603008 | tf_op jit(solution)/shard_map/pack_gate/pallas_call | solution.py:193
  214.6 0.0 copy-start
  214.6 113.4 %all-to-all-done.1.in_ref = bf16[8,16,176,256]{3,2,1,0:T(8,128)(2,1)} async-done(((bf16[8,16,176,256]{3,2,1,0:T(8,128)(2,1)}), bf16[8,16,176,256]{3,2,1,0:T(8,128)(2,1)}, u32[]{:S(2)}, u32[]{:S(2)}) %all-to-all-start.1) | async-done | bytes 11534368 | tf_op jit(solution)/shard_map/all_to_all | solution.py:236
  328.0 5.2 %all-to-all-start = ((bf16[8,16,176,256]{3,2,1,0:T(8,128)(2,1)}), bf16[8,16,176,256]{3,2,1,0:T(8,128)(2,1)}, u32[]{:S(2)}, u32[]{:S(2)}) async-start(bf16[8,16,176,256]{3,2,1,0:T(8,128)(2,1)} %pack_gate.1), calls=%async_computation | async-start | bytes 23068672 | tf_op jit(solution)/shard_map/all_to_all | solution.py:236
  333.3 0.0 copy-done
  333.3 0.1 copy.12
  333.4 0.8 copy.13
  334.1 1.5 fusion.1
  335.6 9.0 %place_down.1 = bf16[16,176,2048]{2,1,0:T(8,128)(2,1)} custom-call(bf16[8,16,176,256]{3,2,1,0:T(8,128)(2,1)} %all-to-all-done.2.in_ref), custom_call_target="tpu_custom_call" | custom-call | flops 5767168 | bytes 23068672 | tf_op jit(solution)/shard_map/place_down/pallas_call | solution.py:217
  344.6 9.0 %place_up.1 = bf16[16,176,2048]{2,1,0:T(8,128)(2,1)} custom-call(bf16[8,16,176,256]{3,2,1,0:T(8,128)(2,1)} %all-to-all-done.1.in_ref), custom_call_target="tpu_custom_call" | custom-call | flops 5767168 | bytes 23068672 | tf_op jit(solution)/shard_map/place_up/pallas_call | solution.py:217
  353.7 107.4 %all-to-all-done.in_ref = bf16[8,16,176,256]{3,2,1,0:T(8,128)(2,1)} async-done(((bf16[8,16,176,256]{3,2,1,0:T(8,128)(2,1)}), bf16[8,16,176,256]{3,2,1,0:T(8,128)(2,1)}, u32[]{:S(2)}, u32[]{:S(2)}) %all-to-all-start) | async-done | bytes 11534368 | tf_op jit(solution)/shard_map/all_to_all | solution.py:236
  461.0 9.0 %place_gate.1 = bf16[16,176,2048]{2,1,0:T(8,128)(2,1)} custom-call(bf16[8,16,176,256]{3,2,1,0:T(8,128)(2,1)} %all-to-all-done.in_ref), custom_call_target="tpu_custom_call" | custom-call | flops 5767168 | bytes 23068672 | tf_op jit(solution)/shard_map/place_gate/pallas_call | solution.py:217
Async XLA Ops:
  62.0 133.0 %all-to-all-start.2 = ((bf16[8,16,176,256]{3,2,1,0:T(8,128)(2,1)}), bf16[8,16,176,256]{3,2,1,0:T(8,128)(2,1)}, u32[]{:S(2)}, u32[]{:S(2)}) async-start(bf16[8,16,176,256]{3,2,1,0:T(8,128)(2,1)} %pack_down.1), calls=%async_computation.2 | async-start | bytes 23068672 | tf_op jit(solution)/shard_map/all_to_all | solution.py:236
  195.0 133.0 %all-to-all-start.1 = ((bf16[8,16,176,256]{3,2,1,0:T(8,128)(2,1)}), bf16[8,16,176,256]{3,2,1,0:T(8,128)(2,1)}, u32[]{:S(2)}, u32[]{:S(2)}) async-start(bf16[8,16,176,256]{3,2,1,0:T(8,128)(2,1)} %pack_up.1), calls=%async_computation.1 | async-start | bytes 23068672 | tf_op jit(solution)/shard_map/all_to_all | solution.py:236
  214.6 118.7 %copy-start = (bf16[4,8,16,256]{3,2,1,0:T(8,128)(2,1)S(1)}, bf16[4,8,16,256]{3,2,1,0:T(8,128)(2,1)}, u32[]{:S(2)}) copy-start(bf16[4,8,16,256]{3,2,1,0:T(8,128)(2,1)} %get-tuple-element.10) | copy-start | bytes 786436
  328.0 133.0 %all-to-all-start = ((bf16[8,16,176,256]{3,2,1,0:T(8,128)(2,1)}), bf16[8,16,176,256]{3,2,1,0:T(8,128)(2,1)}, u32[]{:S(2)}, u32[]{:S(2)}) async-start(bf16[8,16,176,256]{3,2,1,0:T(8,128)(2,1)} %pack_gate.1), calls=%async_computation | async-start | bytes 23068672 | tf_op jit(solution)/shard_map/all_to_all | solution.py:236
